TPU v7x, 128 devices: a whole 4x4x4 slice. The times are simulated.
128 devices in a mesh: case: 1, ens: 128 (over z, y, x, core).
Axes of the slice: x: 4, y: 4, z: 4, core: 2. Of those that a mesh axis runs over, the one named last changes fastest.
Arguments:
- x_init: float32 [128, 512, 69], P(('case', 'ens'))
- a_mix: bfloat16 [512, 512], replicated
- w_in: bfloat16 [4, 69, 512], replicated
- w_out: bfloat16 [4, 512, 69], replicated
- y_obs: float32 [8, 512, 8], P(None, ('case', 'ens'))
- r_inv: float32 [512, 7, 8], P(('case', 'ens'))
- obs_idx: int32 [8], replicated
Outputs:
- output: float32 [128, 512, 69], P(('case', 'ens'))
All inputs are finite; a program needn't handle non-finite values.
Results may differ from a plain program's by a relative error of at most 0.00935664.
Values are sent between devices in bfloat16 or wider.
A program may use at most 1 GiB of HBM per device.

v0:
```python
import math
import jax
import jax.numpy as jnp
from jax import lax
from jax.sharding import PartitionSpec as P

INFLATION = 1.2
NS_STEPS = 16
FULL_PRECISION = lax.Precision.HIGHEST


def value_a8(state, a_mix, w_in, w_out):
    num_cols = state.shape[0]
    num_vars = state.shape[-1]
    for layer in range(w_in.shape[0]):
        flat = state.astype(jnp.bfloat16).reshape(num_cols, -1)
        mixed = jnp.dot(a_mix, flat, preferred_element_type=jnp.float32).astype(jnp.bfloat16)
        hidden = jnp.dot(mixed.reshape(-1, num_vars), w_in[layer], preferred_element_type=jnp.float32)
        hidden_act = jax.nn.gelu(hidden, approximate=True).astype(jnp.bfloat16)
        state = state + jnp.dot(hidden_act, w_out[layer], preferred_element_type=jnp.float32).reshape(state.shape)
    return state


def analysis_weights(win_pert, win_wt, win_innov):
    num_mem = win_pert.shape[2]
    identity = jnp.eye(num_mem, dtype=jnp.float32)
    weighted = win_pert * win_wt[:, :, None, :]
    gram = jnp.einsum('bokp,bolp->bkl', weighted, win_pert, precision=FULL_PRECISION)
    drive = jnp.einsum('bokp,bop->bk', weighted, win_innov, precision=FULL_PRECISION)
    precision_mat = (num_mem - 1) / INFLATION * identity + gram
    trace_val = jnp.trace(precision_mat, axis1=1, axis2=2)
    iter_y = precision_mat / trace_val[:, None, None]
    iter_z = jnp.broadcast_to(identity, precision_mat.shape)
    for _ in range(NS_STEPS):
        factor = 0.5 * (3.0 * identity - jnp.einsum('bij,bjk->bik', iter_z, iter_y, precision=FULL_PRECISION))
        iter_y = jnp.einsum('bij,bjk->bik', iter_y, factor, precision=FULL_PRECISION)
        iter_z = jnp.einsum('bij,bjk->bik', factor, iter_z, precision=FULL_PRECISION)
    inv_root = iter_z / jnp.sqrt(trace_val)[:, None, None]
    inner = jnp.einsum('bij,bj->bi', inv_root, drive, precision=FULL_PRECISION)
    mean_w = jnp.einsum('bij,bj->bi', inv_root, inner, precision=FULL_PRECISION)
    return math.sqrt(num_mem - 1) * inv_root + mean_w[:, :, None]


def local_analysis(col_state, obs_now, r_blk, obs_idx, num_dev):
    num_blk, num_mem, num_vars = col_state.shape
    halo = (r_blk.shape[1] - 1) // 2
    ens_mean = jnp.mean(col_state, axis=1)
    pert = col_state - ens_mean[:, None, :]
    obs_pert = jnp.take(pert, obs_idx, axis=2)
    innovation = obs_now - jnp.take(ens_mean, obs_idx, axis=1)
    pack = jnp.concatenate([obs_pert, innovation[:, None, :]], axis=1)
    to_next = [(src, (src + 1) % num_dev) for src in range(num_dev)]
    to_prev = [(src, (src - 1) % num_dev) for src in range(num_dev)]
    from_left = lax.ppermute(pack[num_blk - halo:], 'ens', to_next)
    from_right = lax.ppermute(pack[:halo], 'ens', to_prev)
    extended = jnp.concatenate([from_left, pack, from_right], axis=0)
    window = jnp.stack([extended[offset:offset + num_blk] for offset in range(2 * halo + 1)], axis=1)
    weights = analysis_weights(window[:, :, :num_mem], r_blk, window[:, :, num_mem])
    update = jnp.einsum('bik,biv->bkv', weights, pert, precision=FULL_PRECISION)
    return ens_mean[:, None, :] + update


def solution(mesh):
    num_dev = mesh.shape['ens']
    def local_run(x_blk, a_mix, w_in, w_out, y_blk, r_blk, obs_idx):
        state = jnp.transpose(x_blk, (1, 0, 2))
        for cycle in range(y_blk.shape[0]):
            state = value_a8(state, a_mix, w_in, w_out)
            col_state = lax.all_to_all(state, 'ens', 0, 1, tiled=True)
            col_state = local_analysis(col_state, y_blk[cycle], r_blk, obs_idx, num_dev)
            state = lax.all_to_all(col_state, 'ens', 1, 0, tiled=True)
        return jnp.transpose(state, (1, 0, 2))
    row_spec = P(('case', 'ens'), None, None)
    return jax.shard_map(local_run, mesh=mesh, in_specs=(row_spec, P(), P(), P(), P(None, ('case', 'ens'), None), row_spec, P()), out_specs=row_spec, check_vma=False)
```

profile of v0, /device:TPU:1, one launch (start us, length us, event | category | flops | bytes accessed | tf_op | source)
XLA Modules:
  0.0 572.8 jit_solution(14326244444644430354)
XLA Ops:
  0.0 1.9 fusion.666
  8.6 11.5 %all-to-all-start = ((f32[512,1,69]{2,1,0:T(1,128)}), f32[512,1,69]{2,1,0:T(1,128)S(1)}, u32[]{:S(2)}, u32[]{:S(2)}) async-start(f32[512,1,69]{2,1,0:T(1,128)} %copy.403), calls=%async_computation | async-start | bytes 524288 | tf_op jit(solution)/shard_map/all_to_all | solution.py:69
  21.0 10.0 %all-to-all-done = f32[512,1,69]{2,1,0:T(1,128)S(1)} async-done(((f32[512,1,69]{2,1,0:T(1,128)}), f32[512,1,69]{2,1,0:T(1,128)S(1)}, u32[]{:S(2)}, u32[]{:S(2)}) %all-to-all-start) | async-done | bytes 141344 | tf_op jit(solution)/shard_map/all_to_all | solution.py:69
  33.7 1.5 collective-permute-start
  58.7 22.0 %all_to_all.285 = f32[4,128,69]{2,0,1:T(4,128)S(1)} all-to-all(f32[4,128,69]{2,0,1:T(4,128)S(1)} %copy.419), channel_id=1, replica_groups=mesh['case'=1,'ens'=128] {'ens'}, dimensions={1} | all-to-all | bytes 282624 | tf_op jit(solution)/shard_map/all_to_all | solution.py:71
  86.0 4.3 all-to-all-start.2
  90.4 10.8 %all-to-all-done.2 = f32[512,1,69]{2,1,0:T(1,128)S(1)} async-done(((f32[512,1,69]{2,1,0:T(1,128)}), f32[512,1,69]{2,1,0:T(1,128)S(1)}, u32[]{:S(2)}, u32[]{:S(2)}) %all-to-all-start.2) | async-done | bytes 141344 | tf_op jit(solution)/shard_map/all_to_all | solution.py:69
  105.2 1.3 collective-permute-done.3
  129.2 21.7 %all_to_all.286 = f32[4,128,69]{2,0,1:T(4,128)S(1)} all-to-all(f32[4,128,69]{2,0,1:T(4,128)S(1)} %copy.436), channel_id=1, replica_groups=mesh['case'=1,'ens'=128] {'ens'}, dimensions={1} | all-to-all | bytes 282624 | tf_op jit(solution)/shard_map/all_to_all | solution.py:71
  156.2 4.3 all-to-all-start.4
  160.6 10.8 %all-to-all-done.4 = f32[512,1,69]{2,1,0:T(1,128)S(1)} async-done(((f32[512,1,69]{2,1,0:T(1,128)}), f32[512,1,69]{2,1,0:T(1,128)S(1)}, u32[]{:S(2)}, u32[]{:S(2)}) %all-to-all-start.4) | async-done | bytes 141344 | tf_op jit(solution)/shard_map/all_to_all | solution.py:69
  175.4 1.4 collective-permute-done.5
  199.2 21.7 %all_to_all.287 = f32[4,128,69]{2,0,1:T(4,128)S(1)} all-to-all(f32[4,128,69]{2,0,1:T(4,128)S(1)} %copy.453), channel_id=1, replica_groups=mesh['case'=1,'ens'=128] {'ens'}, dimensions={1} | all-to-all | bytes 282624 | tf_op jit(solution)/shard_map/all_to_all | solution.py:71
  226.2 4.3 all-to-all-start.6
  230.6 10.8 %all-to-all-done.6 = f32[512,1,69]{2,1,0:T(1,128)S(1)} async-done(((f32[512,1,69]{2,1,0:T(1,128)}), f32[512,1,69]{2,1,0:T(1,128)S(1)}, u32[]{:S(2)}, u32[]{:S(2)}) %all-to-all-start.6) | async-done | bytes 141344 | tf_op jit(solution)/shard_map/all_to_all | solution.py:69
  244.2 1.4 collective-permute-start.6
  269.2 21.9 %all_to_all.288 = f32[4,128,69]{2,0,1:T(4,128)S(1)} all-to-all(f32[4,128,69]{2,0,1:T(4,128)S(1)} %copy.470), channel_id=1, replica_groups=mesh['case'=1,'ens'=128] {'ens'}, dimensions={1} | all-to-all | bytes 282624 | tf_op jit(solution)/shard_map/all_to_all | solution.py:71
  296.4 4.3 all-to-all-start.8
  300.8 10.8 %all-to-all-done.8 = f32[512,1,69]{2,1,0:T(1,128)S(1)} async-done(((f32[512,1,69]{2,1,0:T(1,128)}), f32[512,1,69]{2,1,0:T(1,128)S(1)}, u32[]{:S(2)}, u32[]{:S(2)}) %all-to-all-start.8) | async-done | bytes 141344 | tf_op jit(solution)/shard_map/all_to_all | solution.py:69
  315.6 1.3 collective-permute-done.9
  339.6 21.7 %all_to_all.289 = f32[4,128,69]{2,0,1:T(4,128)S(1)} all-to-all(f32[4,128,69]{2,0,1:T(4,128)S(1)} %copy.487), channel_id=1, replica_groups=mesh['case'=1,'ens'=128] {'ens'}, dimensions={1} | all-to-all | bytes 282624 | tf_op jit(solution)/shard_map/all_to_all | solution.py:71
  366.6 4.3 all-to-all-start.10
  371.0 10.8 %all-to-all-done.10 = f32[512,1,69]{2,1,0:T(1,128)S(1)} async-done(((f32[512,1,69]{2,1,0:T(1,128)}), f32[512,1,69]{2,1,0:T(1,128)S(1)}, u32[]{:S(2)}, u32[]{:S(2)}) %all-to-all-start.10) | async-done | bytes 141344 | tf_op jit(solution)/shard_map/all_to_all | solution.py:69
  385.8 1.4 collective-permute-done.11
  409.6 21.7 %all_to_all.290 = f32[4,128,69]{2,0,1:T(4,128)S(1)} all-to-all(f32[4,128,69]{2,0,1:T(4,128)S(1)} %copy.504), channel_id=1, replica_groups=mesh['case'=1,'ens'=128] {'ens'}, dimensions={1} | all-to-all | bytes 282624 | tf_op jit(solution)/shard_map/all_to_all | solution.py:71
  436.6 4.3 all-to-all-start.12
  441.0 10.8 %all-to-all-done.12 = f32[512,1,69]{2,1,0:T(1,128)S(1)} async-done(((f32[512,1,69]{2,1,0:T(1,128)}), f32[512,1,69]{2,1,0:T(1,128)S(1)}, u32[]{:S(2)}, u32[]{:S(2)}) %all-to-all-start.12) | async-done | bytes 141344 | tf_op jit(solution)/shard_map/all_to_all | solution.py:69
  454.5 1.4 collective-permute-start.12
  479.5 21.9 %all_to_all.291 = f32[4,128,69]{2,0,1:T(4,128)S(1)} all-to-all(f32[4,128,69]{2,0,1:T(4,128)S(1)} %copy.521), channel_id=1, replica_groups=mesh['case'=1,'ens'=128] {'ens'}, dimensions={1} | all-to-all | bytes 282624 | tf_op jit(solution)/shard_map/all_to_all | solution.py:71
  506.8 4.3 all-to-all-start.14
  511.2 10.8 %all-to-all-done.14 = f32[512,1,69]{2,1,0:T(1,128)S(1)} async-done(((f32[512,1,69]{2,1,0:T(1,128)}), f32[512,1,69]{2,1,0:T(1,128)S(1)}, u32[]{:S(2)}, u32[]{:S(2)}) %all-to-all-start.14) | async-done | bytes 141344 | tf_op jit(solution)/shard_map/all_to_all | solution.py:69
  549.8 21.8 %all_to_all.292 = f32[4,128,69]{2,0,1:T(4,128)S(1)} all-to-all(f32[4,128,69]{2,0,1:T(4,128)S(1)} %copy.538), channel_id=1, replica_groups=mesh['case'=1,'ens'=128] {'ens'}, dimensions={1} | all-to-all | bytes 282624 | tf_op jit(solution)/shard_map/all_to_all | solution.py:71
  (747 shorter events, 254.7 us)
Async XLA Ops:
  0.0 2.5 copy-start
  0.0 1.9 copy-start.1
  2.5 0.9 copy-start.2
  8.6 11.5 %copy-start.5 = (s32[8]{0:T(128)S(1)}, s32[8]{0:T(128)}, u32[]{:S(2)}) copy-start(s32[8]{0:T(128)} %param.17) | copy-start | bytes 100
  8.6 22.4 %all-to-all-start = ((f32[512,1,69]{2,1,0:T(1,128)}), f32[512,1,69]{2,1,0:T(1,128)S(1)}, u32[]{:S(2)}, u32[]{:S(2)}) async-start(f32[512,1,69]{2,1,0:T(1,128)} %copy.403), calls=%async_computation | async-start | bytes 524288 | tf_op jit(solution)/shard_map/all_to_all | solution.py:69
  20.1 0.7 copy-start.3
  32.9 2.3 copy-start.4
  32.9 3.3 collective-permute-start.1
  33.7 2.6 collective-permute-start
  86.0 15.2 %all-to-all-start.2 = ((f32[512,1,69]{2,1,0:T(1,128)}), f32[512,1,69]{2,1,0:T(1,128)S(1)}, u32[]{:S(2)}, u32[]{:S(2)}) async-start(f32[512,1,69]{2,1,0:T(1,128)} %copy.421), calls=%async_computation.2 | async-start | bytes 524288 | tf_op jit(solution)/shard_map/all_to_all | solution.py:69
  103.2 3.3 collective-permute-start.3
  103.9 2.6 collective-permute-start.2
  156.2 15.2 %all-to-all-start.4 = ((f32[512,1,69]{2,1,0:T(1,128)}), f32[512,1,69]{2,1,0:T(1,128)S(1)}, u32[]{:S(2)}, u32[]{:S(2)}) async-start(f32[512,1,69]{2,1,0:T(1,128)} %copy.438), calls=%async_computation.4 | async-start | bytes 524288 | tf_op jit(solution)/shard_map/all_to_all | solution.py:69
  173.4 3.3 collective-permute-start.5
  174.2 2.6 collective-permute-start.4
  226.2 15.2 %all-to-all-start.6 = ((f32[512,1,69]{2,1,0:T(1,128)}), f32[512,1,69]{2,1,0:T(1,128)S(1)}, u32[]{:S(2)}, u32[]{:S(2)}) async-start(f32[512,1,69]{2,1,0:T(1,128)} %copy.455), calls=%async_computation.6 | async-start | bytes 524288 | tf_op jit(solution)/shard_map/all_to_all | solution.py:69
  243.4 3.3 collective-permute-start.7
  244.2 2.6 collective-permute-start.6
  296.4 15.2 %all-to-all-start.8 = ((f32[512,1,69]{2,1,0:T(1,128)}), f32[512,1,69]{2,1,0:T(1,128)S(1)}, u32[]{:S(2)}, u32[]{:S(2)}) async-start(f32[512,1,69]{2,1,0:T(1,128)} %copy.472), calls=%async_computation.8 | async-start | bytes 524288 | tf_op jit(solution)/shard_map/all_to_all | solution.py:69
  313.6 3.3 collective-permute-start.9
  314.3 2.6 collective-permute-start.8
  366.6 15.2 %all-to-all-start.10 = ((f32[512,1,69]{2,1,0:T(1,128)}), f32[512,1,69]{2,1,0:T(1,128)S(1)}, u32[]{:S(2)}, u32[]{:S(2)}) async-start(f32[512,1,69]{2,1,0:T(1,128)} %copy.489), calls=%async_computation.10 | async-start | bytes 524288 | tf_op jit(solution)/shard_map/all_to_all | solution.py:69
  383.8 3.3 collective-permute-start.11
  384.6 2.6 collective-permute-start.10
  436.6 15.2 %all-to-all-start.12 = ((f32[512,1,69]{2,1,0:T(1,128)}), f32[512,1,69]{2,1,0:T(1,128)S(1)}, u32[]{:S(2)}, u32[]{:S(2)}) async-start(f32[512,1,69]{2,1,0:T(1,128)} %copy.506), calls=%async_computation.12 | async-start | bytes 524288 | tf_op jit(solution)/shard_map/all_to_all | solution.py:69
  453.8 3.3 collective-permute-start.13
  454.5 2.6 collective-permute-start.12
  506.8 15.2 %all-to-all-start.14 = ((f32[512,1,69]{2,1,0:T(1,128)}), f32[512,1,69]{2,1,0:T(1,128)S(1)}, u32[]{:S(2)}, u32[]{:S(2)}) async-start(f32[512,1,69]{2,1,0:T(1,128)} %copy.523), calls=%async_computation.14 | async-start | bytes 524288 | tf_op jit(solution)/shard_map/all_to_all | solution.py:69
  524.0 3.3 collective-permute-start.15
  524.7 2.6 collective-permute-start.14
where the time goes:
time: 578 us; the launch traced here: 573 us
  matrix products  207 us (36%)
  blocking collectives  175 us (30%)
  waiting for transfers between devices  95.4 us (17%)
  starting transfers between devices  58.1 us (10%)
  local copies, waits for them, and re-layouts  28.9 us (5%)
    all_to_all x8, blocking collectives, local_run(): state = lax.all_to_all(col_state, 'ens', 1, 0, tiled=True)  175 us
    all_to_all x8, waiting for transfers between devices, local_run(): col_state = lax.all_to_all(state, 'ens', 0, 1, tiled=True)  85.5 us
    dot_general x128, matrix products, analysis_weights(): jnp.einsum('bij,bjk->bik', factor, iter_z, precision=FULL_PRECISION)  52.4 us
    dot_general x128, matrix products, analysis_weights(): jnp.einsum('bij,bjk->bik', iter_z, iter_y, precision=FULL_PRECISION)  51.4 us
    dot_general x120, matrix products, analysis_weights(): jnp.einsum('bij,bjk->bik', iter_y, factor, precision=FULL_PRECISION)  47.7 us
    all_to_all x8, starting transfers between devices, local_run(): col_state = lax.all_to_all(state, 'ens', 0, 1, tiled=True)  41.7 us
    dot_general x32, matrix products, value_a8(): jnp.dot(mixed.reshape(-1, num_vars), w_in[layer], preferred_element_type=...  25.4 us
  transfers between devices with their start and end apart: 24, of which 16 were waited for; matrix products, arithmetic and copies ran while one was open for 0% of the time, Pallas kernels for 0%

commit v1 on v0

v1 whole, which is shorter than its diff:
```python
import functools
import math
import jax
import jax.numpy as jnp
from jax import lax
from jax.experimental import pallas as pl
from jax.experimental.pallas import tpu as pltpu
from jax.sharding import PartitionSpec as P

INFLATION = 1.2
NS_STEPS = 16
FULL = lax.Precision.HIGHEST
MESH = pl.DeviceIdType.MESH
BF16 = jnp.bfloat16
F32 = jnp.float32
LANES = 128
PREV_LANE = 72
NEXT_LANE = 96
GAIN_LANE = 127


def split3(x):
    hi = x.astype(BF16)
    rest = x - hi.astype(F32)
    mid = rest.astype(BF16)
    lo = (rest - mid.astype(F32)).astype(BF16)
    return hi, mid, lo


def lhs_pack(x):
    hi, mid, lo = split3(x)
    return jnp.concatenate([hi, mid, hi, mid, hi, lo], axis=1)


def rhs_pack(x):
    hi, mid, lo = split3(x)
    return jnp.concatenate([hi, hi, mid, mid, lo, hi], axis=0)


def dot32(lhs, rhs):
    return jnp.dot(lhs, rhs, preferred_element_type=F32)


def kernel(num_dev, num_cycles, num_obs, halo,
           obs_ref, x_ref, a_ref, win_ref, wout_ref, y_ref, r_ref,
           out_ref,
           state, win_s, wout_s, send1, land1, send2, land2, xz, yprev, ynext, yall,
           s1, r1, s2, r2, sy0, ry0, sy1, ry1):
    me = lax.axis_index('ens')
    num_cols, num_vars = x_ref.shape
    num_layers = win_ref.shape[0]
    blk = num_cols // num_dev
    num_mem = num_dev

    bar = pltpu.get_barrier_semaphore()
    def greet(i, carry):
        pl.semaphore_signal(bar, inc=1, device_id={'ens': lax.rem(me + i, num_dev)}, device_id_type=MESH)
        return carry
    lax.fori_loop(1, num_dev, greet, 0)

    var = lax.broadcasted_iota(jnp.int32, (LANES, LANES), 0)
    lane = lax.broadcasted_iota(jnp.int32, (LANES, LANES), 1)
    place = var + num_obs
    for i in range(num_obs):
        place = place - jnp.where(var > obs_ref[i], 1, 0)
    for i in range(num_obs):
        place = jnp.where(var == obs_ref[i], i, place)
    to_lane = jnp.where((place == lane) & (var < num_vars), 1.0, 0.0).astype(F32)
    to_lane_b = to_lane.astype(BF16)
    eye = jnp.where(var == lane, 1.0, 0.0).astype(F32)

    state[...] = jnp.dot(x_ref[...], to_lane[:num_vars], precision=FULL, preferred_element_type=F32)
    for l in range(num_layers):
        win_s[l] = lax.dot_general(to_lane_b[:num_vars], win_ref[l], (((0,), (0,)), ((), ())),
                                   preferred_element_type=F32).astype(BF16)
        wout_s[l] = jnp.dot(wout_ref[l], to_lane_b[:num_vars], preferred_element_type=F32).astype(BF16)

    send1_rows = send1.reshape(num_cols, LANES)
    land1_rows = land1.reshape(num_mem * blk, LANES)
    send2_rows = send2.reshape(num_mem * blk, LANES)
    land2_rows = land2.reshape(num_cols, LANES)

    def scatter(src, dst, ss, rs):
        def body(i, carry):
            peer = lax.rem(me + i, num_dev)
            pltpu.make_async_remote_copy(src_ref=src.at[peer], dst_ref=dst.at[me], send_sem=ss, recv_sem=rs,
                                         device_id={'ens': peer}, device_id_type=MESH).start()
            return carry
        lax.fori_loop(1, num_dev, body, 0)
        dst[pl.ds(me, 1)] = src[pl.ds(me, 1)]

    def settle(src, dst, ss, rs):
        pltpu.make_async_copy(src.at[pl.ds(0, num_dev - 1)], dst.at[pl.ds(0, num_dev - 1)], ss).wait()
        pltpu.make_async_copy(src.at[pl.ds(0, num_dev - 1)], dst.at[pl.ds(0, num_dev - 1)], rs).wait()

    def y_copies():
        right = lax.rem(me + 1, num_dev)
        left = lax.rem(me + num_dev - 1, num_dev)
        return (pltpu.make_async_remote_copy(src_ref=y_ref, dst_ref=yprev, send_sem=sy0, recv_sem=ry0,
                                             device_id={'ens': right}, device_id_type=MESH),
                pltpu.make_async_remote_copy(src_ref=y_ref, dst_ref=ynext, send_sem=sy1, recv_sem=ry1,
                                             device_id={'ens': left}, device_id_type=MESH))

    TILE = 128
    def forecast():
        for l in range(num_layers):
            hb = state[...].astype(BF16)
            for t in range(num_cols // TILE):
                rows = pl.ds(t * TILE, TILE)
                mixed = jnp.dot(a_ref[rows, :], hb, preferred_element_type=F32).astype(BF16)
                hidden = jnp.dot(mixed, win_s[l], preferred_element_type=F32)
                act = jax.nn.gelu(hidden, approximate=True).astype(BF16)
                state[rows, :] += jnp.dot(act, wout_s[l], preferred_element_type=F32)

    lane_row = lax.broadcasted_iota(jnp.int32, (num_cols, LANES), 1)
    col_row = lax.broadcasted_iota(jnp.int32, (num_cols, LANES), 0) % blk

    def pack_state():
        h = state[...]
        before = pltpu.roll(h, blk, 0)
        after = pltpu.roll(h, num_cols - blk, 0)
        res = h
        for n in range(2 * halo):
            if n < halo:
                col, src, lane0 = (n - halo) % blk, before, PREV_LANE + n * num_obs
            else:
                col, src, lane0 = n - halo, after, NEXT_LANE + (n - halo) * num_obs
            moved = pltpu.roll(src, lane0, 1)
            here = (lane_row >= lane0) & (lane_row < lane0 + num_obs)
            res = jnp.where(here, jnp.where(col_row == col, moved, 0.0), res)
        send1_rows[...] = res

    mem_lane = lax.broadcasted_iota(jnp.int32, (num_mem, LANES), 1)

    def analyse(cycle):
        raws = [land1_rows[pl.ds(j, num_mem, stride=blk), :] for j in range(blk)]
        halo_sum = raws[0]
        for j in range(1, blk):
            halo_sum = halo_sum + raws[j]
        own = raws[0]
        for j in range(1, blk):
            own = jnp.where(mem_lane >= j * num_obs, pltpu.roll(raws[j], j * num_obs, 1), own)
        obs_raw = jnp.where(mem_lane < blk * num_obs, own, halo_sum)
        unused = ((mem_lane >= blk * num_obs) & (mem_lane < PREV_LANE)) | (mem_lane >= NEXT_LANE + halo * num_obs)
        obs_raw = jnp.where(unused, 0.0, obs_raw)
        obs_mean = jnp.mean(obs_raw, axis=0, keepdims=True)
        pert = obs_raw - obs_mean
        innov = yall[pl.ds(cycle, 1), :] - obs_mean
        r_all = r_ref[...]
        energy = jnp.sum(pert * pert, axis=0, keepdims=True)
        base = (num_mem - 1) / INFLATION
        trace = num_mem * base + jnp.sum(r_all * energy, axis=1, keepdims=True)
        innov_rows = jnp.where(lax.broadcasted_iota(jnp.int32, (LANES, LANES), 0) == GAIN_LANE, innov, 0.0)
        right = jnp.concatenate([pert, innov_rows], axis=0)
        means = []
        for j in range(blk):
            weighted = pert * r_all[j:j + 1]
            res = lax.dot_general(weighted, right, (((1,), (1,)), ((), ())), precision=FULL, preferred_element_type=F32)
            inv = 1.0 / trace[j:j + 1]
            xz[j, :, :LANES] = (res[:, :LANES] + base * eye) * inv
            mean = jnp.mean(raws[j], axis=0, keepdims=True)
            means.append(mean)
            xz[j, :, LANES:] = jnp.where(mem_lane < num_vars, raws[j] - mean, res[:, LANES:])

        def ns_step(k, carry):
            for j in range(blk):
                both = xz[j]
                factor = 1.5 * eye - 0.5 * both[:, :LANES]
                lhs = lhs_pack(factor)
                first = dot32(lhs, rhs_pack(both))
                xz[j, :, LANES:] = first[:, LANES:]
                xz[j, :, :LANES] = dot32(lhs, rhs_pack(first[:, :LANES]))
            return carry
        lax.fori_loop(0, NS_STEPS - 1, ns_step, 0)

        for j in range(blk):
            factor = 1.5 * eye - 0.5 * xz[j, :, :LANES]
            fin = dot32(lhs_pack(factor), rhs_pack(xz[j, :, LANES:]))
            inv = 1.0 / trace[j:j + 1]
            shift = jnp.sum(fin * fin[:, GAIN_LANE:GAIN_LANE + 1], axis=0, keepdims=True) * inv
            new = means[j] + shift + (math.sqrt(num_mem - 1) * jnp.sqrt(inv)) * fin
            send2_rows[pl.ds(j, num_mem, stride=blk), :] = jnp.where(mem_lane < num_vars, new, 0.0)

    def cycle_body(cycle, carry):
        forecast()
        pack_state()
        @pl.when(cycle == 0)
        def _():
            pl.semaphore_wait(bar, num_dev - 1)
            for copy in y_copies():
                copy.start()
        scatter(send1, land1, s1, r1)
        @pl.when(cycle == 0)
        def _():
            for copy in y_copies():
                copy.wait()
            ylane = lax.broadcasted_iota(jnp.int32, (num_cycles, LANES), 1)
            width = halo * num_obs
            prev = pltpu.roll(yprev[...], PREV_LANE - (blk - halo) * num_obs, 1)
            nxt = pltpu.roll(ynext[...], NEXT_LANE, 1)
            full = y_ref[...]
            full = jnp.where((ylane >= PREV_LANE) & (ylane < PREV_LANE + width), prev, full)
            full = jnp.where((ylane >= NEXT_LANE) & (ylane < NEXT_LANE + width), nxt, full)
            yall[...] = full
        settle(send1, land1, s1, r1)
        analyse(cycle)
        scatter(send2, land2, s2, r2)
        settle(send2, land2, s2, r2)
        state[...] = land2_rows[...]
        return carry
    lax.fori_loop(0, num_cycles, cycle_body, 0)

    final = lax.dot_general(state[...], to_lane, (((1,), (1,)), ((), ())), precision=FULL, preferred_element_type=F32)
    out_ref[...] = final[:, :num_vars]


def solution(mesh):
    num_dev = mesh.shape['ens']

    def local_run(x_blk, a_mix, w_in, w_out, y_blk, r_blk, obs_idx):
        _, num_cols, num_vars = x_blk.shape
        num_cycles, blk, num_obs = y_blk.shape
        halo = (r_blk.shape[1] - 1) // 2
        num_layers, _, num_hid = w_in.shape
        y_flat = jnp.pad(y_blk.reshape(num_cycles, blk * num_obs), ((0, 0), (0, LANES - blk * num_obs)))
        spread = jnp.stack([jnp.pad(r_blk[j], ((j, blk - 1 - j), (0, 0))) for j in range(blk)])
        spread = spread.reshape(blk, (blk + 2 * halo) * num_obs)
        width = halo * num_obs
        prev, own, nxt = spread[:, :width], spread[:, width:width + blk * num_obs], spread[:, width + blk * num_obs:]
        r_all = jnp.concatenate([
            own, jnp.zeros((blk, PREV_LANE - blk * num_obs), F32), prev,
            jnp.zeros((blk, NEXT_LANE - PREV_LANE - width), F32), nxt,
            jnp.zeros((blk, LANES - NEXT_LANE - width), F32)], axis=1)
        vmem = pl.BlockSpec(memory_space=pltpu.VMEM)
        block = pltpu.VMEM((num_dev, blk, LANES), F32)
        out = pl.pallas_call(
            functools.partial(kernel, num_dev, num_cycles, num_obs, halo),
            out_shape=jax.ShapeDtypeStruct((num_cols, num_vars), F32),
            in_specs=[pl.BlockSpec(memory_space=pltpu.SMEM)] + [vmem] * 6,
            out_specs=vmem,
            scratch_shapes=[
                pltpu.VMEM((num_cols, LANES), F32),
                pltpu.VMEM((num_layers, LANES, num_hid), BF16),
                pltpu.VMEM((num_layers, num_hid, LANES), BF16),
                block, block, block, block,
                pltpu.VMEM((blk, num_dev, 2 * LANES), F32),
                pltpu.VMEM((num_cycles, LANES), F32),
                pltpu.VMEM((num_cycles, LANES), F32),
                pltpu.VMEM((num_cycles, LANES), F32),
            ] + [pltpu.SemaphoreType.DMA] * 8,
            compiler_params=pltpu.CompilerParams(collective_id=0, has_side_effects=True),
        )(obs_idx, x_blk[0], a_mix, w_in, w_out, y_flat, r_all)
        return out[None]

    row_spec = P(('case', 'ens'), None, None)
    return jax.shard_map(local_run, mesh=mesh,
                         in_specs=(row_spec, P(), P(), P(), P(None, ('case', 'ens'), None), row_spec, P()),
                         out_specs=row_spec, check_vma=False)
```

time: 578 us -> 311 us (0.54)
  Pallas kernels: 0 us -> 304 us
  matrix products: 207 us -> 0 us
  blocking collectives: 175 us -> 0 us
  waiting for transfers between devices: 95.4 us -> 0 us
  starting transfers between devices: 58.1 us -> 0 us
  local copies, waits for them, and re-layouts: 28.9 us -> 7.33 us
    pallas_call x0 -> x1, Pallas kernels: none -> 304 us  [local_run(): pl.pallas_call(functools.partial(kernel, num_dev, num_cycles, num_obs, ha...]
    dot_general x480 -> x0, matrix products: 207 us -> none  [the longest x128 52.4 us: analysis_weights(): jnp.einsum('bij,bjk->bik', factor, iter_z, precision=FULL_PRECISION)]
    all_to_all x8 -> x0, blocking collectives: 175 us -> none  [local_run(): state = lax.all_to_all(col_state, 'ens', 1, 0, tiled=True)]
    all_to_all x8 -> x0, waiting for transfers between devices: 85.5 us -> none  [local_run(): col_state = lax.all_to_all(state, 'ens', 0, 1, tiled=True)]
    all_to_all x8 -> x0, starting transfers between devices: 41.7 us -> none  [local_run(): col_state = lax.all_to_all(state, 'ens', 0, 1, tiled=True)]
    ppermute x16 -> x0, starting transfers between devices: 16.4 us -> none  [the longest x8 10.5 us: local_analysis(): from_left = lax.ppermute(pack[num_blk - halo:], 'ens', to_next)]
    ppermute x16 -> x0, waiting for transfers between devices: 9.95 us -> none  [the longest x8 9.92 us: local_analysis(): from_right = lax.ppermute(pack[:halo], 'ens', to_prev)]
    gather x16 -> x0, local copies, waits for them, and re-layouts: 9.05 us -> none  [the longest x8 4.6 us: local_analysis(): obs_pert = jnp.take(pert, obs_idx, axis=2)]
  transfers between devices with their start and end apart: 24 -> 0, of which waited for: 16 -> 0; matrix products, arithmetic and copies ran while one was open for 0% -> 0% of each run, Pallas kernels for 0% -> 0%
where the time goes in v1:
time: 311 us
  Pallas kernels  304 us (98%)
  local copies, waits for them, and re-layouts  7.33 us (2%)
    pallas_call x1, Pallas kernels, local_run(): pl.pallas_call(functools.partial(kernel, num_dev, num_cycles, num_obs, ha...  304 us

profile of v1, /device:TPU:1, one launch (start us, length us, event | category | flops | bytes accessed | tf_op | source)
XLA Modules:
  0.0 311.2 jit_solution(2281962699206121071)
XLA Ops:
  0.0 0.0 copy-start.3
  0.0 0.0 copy-start.2
  0.0 0.8 reshape.12
  0.8 0.6 pad.20.y_ref
  1.4 0.0 copy-done.3
  1.5 0.0 copy-start
  1.5 0.1 stack.16
  1.6 0.1 stack.15
  1.7 0.1 stack.18
  1.8 0.1 stack.17
  1.9 0.1 slice.25
  2.0 0.1 fusion.1
  2.0 0.7 concatenate.4.r_ref
  2.7 0.0 copy-done.2
  2.7 0.8 copy.16
  3.5 0.0 copy-done
  3.5 0.0 copy-start.1
  3.5 0.8 copy.21.win_ref
  4.3 0.2 copy-done.1
  4.6 1.1 copy.22.wout_ref
  5.7 303.8 %shard_map.73 = f32[512,69]{1,0:T(8,128)} custom-call(s32[8]{0:T(128)} %obs_ref.1, f32[512,69]{1,0:T(8,128)} %bitcast.11, bf16[512,512]{1,0:T(8,128)(2,1)} %a_ref.1, bf16[4,69,512]{2,1,0:T(8,128)(2,1)} %copy.21.win_ref, bf16[4,512,69]{2,1,0:T(8,128)(2,1)} %copy.22.wout_ref, f32[8,128]{1,0:T(8,128)} %pad.20.y_ref, f32[4,128]{1,0:T(4,128)} %concatenate.4.r_ref), custom_call_target="tpu_custom_call" | custom-call | tf_op jit(solution)/shard_map/pallas_call | solution.py:236
  309.5 1.7 copy.23
  (10 shorter events, 0.1 us)
Async XLA Ops:
  0.0 1.4 copy-start.3
  0.0 2.7 copy-start.2
  1.5 2.1 copy-start
  3.5 1.0 copy-start.1

commit v2 on v1

--- a/solution.py
+++ b/solution.py
@@ -9,6 +9,7 @@
 
 INFLATION = 1.2
 NS_STEPS = 16
+NS_UNROLL = 3
 FULL = lax.Precision.HIGHEST
 MESH = pl.DeviceIdType.MESH
 BF16 = jnp.bfloat16
@@ -163,15 +164,18 @@
             xz[j, :, LANES:] = jnp.where(mem_lane < num_vars, raws[j] - mean, res[:, LANES:])
 
         def ns_step(k, carry):
-            for j in range(blk):
-                both = xz[j]
-                factor = 1.5 * eye - 0.5 * both[:, :LANES]
-                lhs = lhs_pack(factor)
-                first = dot32(lhs, rhs_pack(both))
-                xz[j, :, LANES:] = first[:, LANES:]
-                xz[j, :, :LANES] = dot32(lhs, rhs_pack(first[:, :LANES]))
+            for _ in range(NS_UNROLL):
+                lhs, first = [], []
+                for j in range(blk):
+                    both = xz[j]
+                    lhs.append(lhs_pack(1.5 * eye - 0.5 * both[:, :LANES]))
+                    res = dot32(lhs[j], rhs_pack(both))
+                    xz[j, :, LANES:] = res[:, LANES:]
+                    first.append(res[:, :LANES])
+                for j in range(blk):
+                    xz[j, :, :LANES] = dot32(lhs[j], rhs_pack(first[j]))
             return carry
-        lax.fori_loop(0, NS_STEPS - 1, ns_step, 0)
+        lax.fori_loop(0, (NS_STEPS - 1) // NS_UNROLL, ns_step, 0)
 
         for j in range(blk):
             factor = 1.5 * eye - 0.5 * xz[j, :, :LANES]

time: 311 us -> 254 us (0.82)
  Pallas kernels: 304 us -> 247 us
    pallas_call x1, Pallas kernels: 304 us -> 247 us  [local_run(): pl.pallas_call(functools.partial(kernel, num_dev, num_cycles, num_obs, ha...]
where the time goes in v2:
time: 254 us
  Pallas kernels  247 us (97%)
  local copies, waits for them, and re-layouts  7.33 us (3%)
    pallas_call x1, Pallas kernels, local_run(): pl.pallas_call(functools.partial(kernel, num_dev, num_cycles, num_obs, ha...  247 us

profile of v2, /device:TPU:1, one launch (start us, length us, event | category | flops | bytes accessed | tf_op | source)
XLA Modules:
  0.0 254.0 jit_solution(9083869956099909244)
XLA Ops:
  0.0 0.0 copy-start.3
  0.0 0.0 copy-start.2
  0.0 0.8 reshape.12
  0.8 0.6 pad.20.y_ref
  1.4 0.0 copy-done.3
  1.5 0.0 copy-start
  1.5 0.1 stack.16
  1.6 0.1 stack.15
  1.7 0.1 stack.18
  1.8 0.1 stack.17
  1.9 0.1 slice.25
  2.0 0.1 fusion.1
  2.0 0.7 concatenate.4.r_ref
  2.7 0.0 copy-done.2
  2.7 0.8 copy.16
  3.5 0.0 copy-done
  3.5 0.0 copy-start.1
  3.5 0.8 copy.21.win_ref
  4.3 0.2 copy-done.1
  4.6 1.1 copy.22.wout_ref
  5.7 246.6 %shard_map.73 = f32[512,69]{1,0:T(8,128)} custom-call(s32[8]{0:T(128)} %obs_ref.1, f32[512,69]{1,0:T(8,128)} %bitcast.11, bf16[512,512]{1,0:T(8,128)(2,1)} %a_ref.1, bf16[4,69,512]{2,1,0:T(8,128)(2,1)} %copy.21.win_ref, bf16[4,512,69]{2,1,0:T(8,128)(2,1)} %copy.22.wout_ref, f32[8,128]{1,0:T(8,128)} %pad.20.y_ref, f32[4,128]{1,0:T(4,128)} %concatenate.4.r_ref), custom_call_target="tpu_custom_call" | custom-call | tf_op jit(solution)/shard_map/pallas_call | solution.py:240
  252.2 1.7 copy.23
  (10 shorter events, 0.1 us)
Async XLA Ops:
  0.0 1.4 copy-start.3
  0.0 2.7 %copy-start.2 = (f32[1,512,69]{1,0,2:T(1,128)S(1)}, f32[1,512,69]{1,0,2:T(1,128)}, u32[]{:S(2)}) copy-start(f32[1,512,69]{1,0,2:T(1,128)} %param.7) | copy-start | bytes 423940
  1.5 2.1 copy-start
  3.5 1.0 copy-start.1

commit v3 on v2

--- a/solution.py
+++ b/solution.py
@@ -1,5 +1,6 @@
 import functools
 import math
+import random
 import jax
 import jax.numpy as jnp
 from jax import lax
@@ -18,6 +19,7 @@
 PREV_LANE = 72
 NEXT_LANE = 96
 GAIN_LANE = 127
+ROWS = 80
 
 
 def split3(x):
@@ -38,6 +40,18 @@
     return jnp.concatenate([hi, hi, mid, mid, lo, hi], axis=0)
 
 
+def far_first(side):
+    offsets = [(z, y, x, c) for z in range(side) for y in range(side) for x in range(side) for c in range(2)][1:]
+    random.Random(1).shuffle(offsets)
+    return sorted(offsets, key=lambda o: -sum(min(d, side - d) for d in o[:3]))
+
+
+def gelu(x):
+    half = 0.5 * x
+    scale = math.sqrt(2 / math.pi)
+    return half + half * jnp.tanh(x * (scale + (scale * 0.044715) * (x * x)))
+
+
 def dot32(lhs, rhs):
     return jnp.dot(lhs, rhs, preferred_element_type=F32)
 
@@ -45,10 +59,10 @@
 def kernel(num_dev, num_cycles, num_obs, halo,
            obs_ref, x_ref, a_ref, win_ref, wout_ref, y_ref, r_ref,
            out_ref,
-           state, win_s, wout_s, send1, land1, send2, land2, xz, yprev, ynext, yall,
+           state, mix_s, win_s, wout_s, send1, land1, send2, land2, xz, yprev, ynext, yall,
            s1, r1, s2, r2, sy0, ry0, sy1, ry1):
     me = lax.axis_index('ens')
-    num_cols, num_vars = x_ref.shape
+    num_vars, num_cols = x_ref.shape
     num_layers = win_ref.shape[0]
     blk = num_cols // num_dev
     num_mem = num_dev
@@ -59,35 +73,46 @@
         return carry
     lax.fori_loop(1, num_dev, greet, 0)
 
-    var = lax.broadcasted_iota(jnp.int32, (LANES, LANES), 0)
-    lane = lax.broadcasted_iota(jnp.int32, (LANES, LANES), 1)
-    place = var + num_obs
-    for i in range(num_obs):
-        place = place - jnp.where(var > obs_ref[i], 1, 0)
-    for i in range(num_obs):
-        place = jnp.where(var == obs_ref[i], i, place)
-    to_lane = jnp.where((place == lane) & (var < num_vars), 1.0, 0.0).astype(F32)
-    to_lane_b = to_lane.astype(BF16)
-    eye = jnp.where(var == lane, 1.0, 0.0).astype(F32)
-
-    state[...] = jnp.dot(x_ref[...], to_lane[:num_vars], precision=FULL, preferred_element_type=F32)
+    def order(dim):
+        var = lax.broadcasted_iota(jnp.int32, (LANES, LANES), dim)
+        slot = lax.broadcasted_iota(jnp.int32, (LANES, LANES), 1 - dim)
+        place = var + num_obs
+        for i in range(num_obs):
+            place = place - jnp.where(var > obs_ref[i], 1, 0)
+        for i in range(num_obs):
+            place = jnp.where(var == obs_ref[i], i, place)
+        return jnp.where((place == slot) & (var < num_vars), 1.0, 0.0).astype(F32)
+    var_slot = order(0)[:num_vars]
+    slot_var = order(1)[:, :num_vars]
+    eye = jnp.where(lax.broadcasted_iota(jnp.int32, (LANES, LANES), 0)
+                    == lax.broadcasted_iota(jnp.int32, (LANES, LANES), 1), 1.0, 0.0).astype(F32)
+    eye_cols = jnp.where(lax.broadcasted_iota(jnp.int32, (num_cols, num_cols), 0)
+                         == lax.broadcasted_iota(jnp.int32, (num_cols, num_cols), 1), 1.0, 0.0).astype(BF16)
+
+    state[...] = jnp.dot(slot_var[:ROWS], x_ref[...], precision=FULL, preferred_element_type=F32)
+    mix_s[...] = lax.dot_general(eye_cols, a_ref[...], (((1,), (1,)), ((), ())),
+                                 preferred_element_type=F32).astype(BF16)
     for l in range(num_layers):
-        win_s[l] = lax.dot_general(to_lane_b[:num_vars], win_ref[l], (((0,), (0,)), ((), ())),
-                                   preferred_element_type=F32).astype(BF16)
-        wout_s[l] = jnp.dot(wout_ref[l], to_lane_b[:num_vars], preferred_element_type=F32).astype(BF16)
+        win_s[l] = jnp.dot(win_ref[l], var_slot.astype(BF16), preferred_element_type=F32).astype(BF16)
+        wout_s[l] = jnp.dot(slot_var[:ROWS].astype(BF16), wout_ref[l], preferred_element_type=F32).astype(BF16)
 
     send1_rows = send1.reshape(num_cols, LANES)
     land1_rows = land1.reshape(num_mem * blk, LANES)
     send2_rows = send2.reshape(num_mem * blk, LANES)
     land2_rows = land2.reshape(num_cols, LANES)
 
+    side = 4
+    chip = me // 2
+    z_at = [(chip // (side * side) + d) % side * (2 * side * side) for d in range(side)]
+    y_at = [(chip // side % side + d) % side * (2 * side) for d in range(side)]
+    x_at = [(chip % side + d) % side * 2 for d in range(side)]
+    c_at = [(me + d) % 2 for d in range(2)]
+
     def scatter(src, dst, ss, rs):
-        def body(i, carry):
-            peer = lax.rem(me + i, num_dev)
+        for dz, dy, dx, dc in far_first(side):
+            peer = z_at[dz] + y_at[dy] + x_at[dx] + c_at[dc]
             pltpu.make_async_remote_copy(src_ref=src.at[peer], dst_ref=dst.at[me], send_sem=ss, recv_sem=rs,
                                          device_id={'ens': peer}, device_id_type=MESH).start()
-            return carry
-        lax.fori_loop(1, num_dev, body, 0)
         dst[pl.ds(me, 1)] = src[pl.ds(me, 1)]
 
     def settle(src, dst, ss, rs):
@@ -105,31 +130,26 @@
     TILE = 128
     def forecast():
         for l in range(num_layers):
-            hb = state[...].astype(BF16)
-            for t in range(num_cols // TILE):
-                rows = pl.ds(t * TILE, TILE)
-                mixed = jnp.dot(a_ref[rows, :], hb, preferred_element_type=F32).astype(BF16)
-                hidden = jnp.dot(mixed, win_s[l], preferred_element_type=F32)
-                act = jax.nn.gelu(hidden, approximate=True).astype(BF16)
-                state[rows, :] += jnp.dot(act, wout_s[l], preferred_element_type=F32)
-
-    lane_row = lax.broadcasted_iota(jnp.int32, (num_cols, LANES), 1)
-    col_row = lax.broadcasted_iota(jnp.int32, (num_cols, LANES), 0) % blk
+            mixed = dot32(state[...].astype(BF16), mix_s[...]).astype(BF16)
+            mixed = jnp.concatenate([mixed, jnp.zeros((LANES - ROWS, num_cols), BF16)], axis=0)
+            acts = []
+            for t in range(win_s.shape[1] // TILE):
+                acts.append(gelu(dot32(win_s[l, pl.ds(t * TILE, TILE), :], mixed)).astype(BF16))
+            state[...] += dot32(wout_s[l], jnp.concatenate(acts, axis=0))
+
+    own_col = lax.broadcasted_iota(jnp.int32, (num_obs, num_cols), 1) % blk
 
     def pack_state():
-        h = state[...]
-        before = pltpu.roll(h, blk, 0)
-        after = pltpu.roll(h, num_cols - blk, 0)
-        res = h
-        for n in range(2 * halo):
-            if n < halo:
-                col, src, lane0 = (n - halo) % blk, before, PREV_LANE + n * num_obs
-            else:
-                col, src, lane0 = n - halo, after, NEXT_LANE + (n - halo) * num_obs
-            moved = pltpu.roll(src, lane0, 1)
-            here = (lane_row >= lane0) & (lane_row < lane0 + num_obs)
-            res = jnp.where(here, jnp.where(col_row == col, moved, 0.0), res)
-        send1_rows[...] = res
+        obs = state[:num_obs, :]
+        before = pltpu.roll(obs, blk, 1)
+        after = pltpu.roll(obs, num_cols - blk, 1)
+        parts = [state[:PREV_LANE, :]]
+        for n in range(halo):
+            parts.append(jnp.where(own_col == (n - halo) % blk, before, 0.0))
+        for n in range(halo):
+            parts.append(jnp.where(own_col == n, after, 0.0))
+        parts.append(jnp.zeros((LANES - PREV_LANE - 2 * halo * num_obs, num_cols), F32))
+        send1_rows[...] = jnp.concatenate(parts, axis=0).T
 
     mem_lane = lax.broadcasted_iota(jnp.int32, (num_mem, LANES), 1)
 
@@ -210,12 +230,11 @@
         analyse(cycle)
         scatter(send2, land2, s2, r2)
         settle(send2, land2, s2, r2)
-        state[...] = land2_rows[...]
+        state[...] = land2_rows[...].T[:ROWS]
         return carry
     lax.fori_loop(0, num_cycles, cycle_body, 0)
 
-    final = lax.dot_general(state[...], to_lane, (((1,), (1,)), ((), ())), precision=FULL, preferred_element_type=F32)
-    out_ref[...] = final[:, :num_vars]
+    out_ref[...] = jnp.dot(var_slot[:, :ROWS], state[...], precision=FULL, preferred_element_type=F32)
 
 
 def solution(mesh):
@@ -239,13 +258,14 @@
         block = pltpu.VMEM((num_dev, blk, LANES), F32)
         out = pl.pallas_call(
             functools.partial(kernel, num_dev, num_cycles, num_obs, halo),
-            out_shape=jax.ShapeDtypeStruct((num_cols, num_vars), F32),
+            out_shape=jax.ShapeDtypeStruct((num_vars, num_cols), F32),
             in_specs=[pl.BlockSpec(memory_space=pltpu.SMEM)] + [vmem] * 6,
             out_specs=vmem,
             scratch_shapes=[
-                pltpu.VMEM((num_cols, LANES), F32),
-                pltpu.VMEM((num_layers, LANES, num_hid), BF16),
+                pltpu.VMEM((ROWS, num_cols), F32),
+                pltpu.VMEM((num_cols, num_cols), BF16),
                 pltpu.VMEM((num_layers, num_hid, LANES), BF16),
+                pltpu.VMEM((num_layers, ROWS, num_hid), BF16),
                 block, block, block, block,
                 pltpu.VMEM((blk, num_dev, 2 * LANES), F32),
                 pltpu.VMEM((num_cycles, LANES), F32),
@@ -253,8 +273,8 @@
                 pltpu.VMEM((num_cycles, LANES), F32),
             ] + [pltpu.SemaphoreType.DMA] * 8,
             compiler_params=pltpu.CompilerParams(collective_id=0, has_side_effects=True),
-        )(obs_idx, x_blk[0], a_mix, w_in, w_out, y_flat, r_all)
-        return out[None]
+        )(obs_idx, x_blk[0].T, a_mix, jnp.swapaxes(w_in, 1, 2), jnp.swapaxes(w_out, 1, 2), y_flat, r_all)
+        return out.T[None]
 
     row_spec = P(('case', 'ens'), None, None)
     return jax.shard_map(local_run, mesh=mesh,

time: 254 us -> 225 us (0.89)
  Pallas kernels: 247 us -> 216 us
    pallas_call x1, Pallas kernels: 247 us -> 216 us  [local_run(): pl.pallas_call(functools.partial(kernel, num_dev, num_cycles, num_obs, ha...]
where the time goes in v3:
time: 225 us; the launch traced here: 224 us
  Pallas kernels  216 us (96%)
  local copies, waits for them, and re-layouts  8.06 us (4%)
    pallas_call x1, Pallas kernels, local_run(): pl.pallas_call(functools.partial(kernel, num_dev, num_cycles, num_obs, ha...  216 us

profile of v3, /device:TPU:1, one launch (start us, length us, event | category | flops | bytes accessed | tf_op | source)
XLA Modules:
  0.0 224.4 jit_solution(857651125897117305)
XLA Ops:
  0.0 0.0 copy-start.2
  0.0 0.0 copy-start
  0.0 0.8 reshape.12
  0.8 0.6 pad.20.y_ref
  1.4 0.0 copy-done.2
  1.5 0.1 stack.16
  1.6 0.1 stack.15
  1.7 0.1 stack.18
  1.8 0.1 stack.17
  1.9 0.1 slice.25
  1.9 0.1 fusion.1
  2.0 0.7 concatenate.4.r_ref
  2.7 1.6 copy.34
  4.3 0.0 copy-done
  4.3 0.0 copy-start.1
  4.3 0.8 copy.33
  5.1 0.2 copy-done.1
  5.3 1.1 copy.15
  6.4 216.3 %shard_map.73 = f32[69,512]{1,0:T(8,128)} custom-call(s32[8]{0:T(128)} %obs_ref.1, f32[69,512]{1,0:T(8,128)} %bitcast.23, bf16[512,512]{1,0:T(8,128)(2,1)} %a_ref.1, bf16[4,512,69]{2,1,0:T(8,128)(2,1)} %bitcast.20, bf16[4,69,512]{2,1,0:T(8,128)(2,1)} %bitcast.21, f32[8,128]{1,0:T(8,128)} %pad.20.y_ref, f32[4,128]{1,0:T(4,128)} %concatenate.4.r_ref), custom_call_target="tpu_custom_call" | custom-call | tf_op jit(solution)/shard_map/pallas_call | solution.py:259
  222.7 1.7 copy.21
  (10 shorter events, 0.1 us)
Async XLA Ops:
  0.0 1.4 copy-start.2
  0.0 4.3 %copy-start = (bf16[4,512,69]{1,0,2:T(4,128)(2,1)S(1)}, bf16[4,512,69]{1,0,2:T(4,128)(2,1)}, u32[]{:S(2)}) copy-start(bf16[4,512,69]{1,0,2:T(4,128)(2,1)} %param.10) | copy-start | bytes 847876
  4.3 1.0 copy-start.1

commit v4 on v3

--- a/solution.py
+++ b/solution.py
@@ -10,7 +10,6 @@
 
 INFLATION = 1.2
 NS_STEPS = 16
-NS_UNROLL = 3
 FULL = lax.Precision.HIGHEST
 MESH = pl.DeviceIdType.MESH
 BF16 = jnp.bfloat16
@@ -46,10 +45,9 @@
     return sorted(offsets, key=lambda o: -sum(min(d, side - d) for d in o[:3]))
 
 
-def gelu(x):
-    half = 0.5 * x
+def gelu_of_double(u):
     scale = math.sqrt(2 / math.pi)
-    return half + half * jnp.tanh(x * (scale + (scale * 0.044715) * (x * x)))
+    return u + u * jnp.tanh(u * (2 * scale + (8 * scale * 0.044715) * (u * u)))
 
 
 def dot32(lhs, rhs):
@@ -57,12 +55,12 @@
 
 
 def kernel(num_dev, num_cycles, num_obs, halo,
-           obs_ref, x_ref, a_ref, win_ref, wout_ref, y_ref, r_ref,
+           obs_ref, x_ref, a_ref, win_ref, wout_ref, y_in, r_in,
            out_ref,
-           state, mix_s, win_s, wout_s, send1, land1, send2, land2, xz, yprev, ynext, yall,
+           state, mix_s, win_s, wout_s, send1, land1, send2, land2, y_ref, yprev, ynext, yall, wide, r_ref,
            s1, r1, s2, r2, sy0, ry0, sy1, ry1):
     me = lax.axis_index('ens')
-    num_vars, num_cols = x_ref.shape
+    num_vars, _, num_cols = x_ref.shape
     num_layers = win_ref.shape[0]
     blk = num_cols // num_dev
     num_mem = num_dev
@@ -89,11 +87,11 @@
     eye_cols = jnp.where(lax.broadcasted_iota(jnp.int32, (num_cols, num_cols), 0)
                          == lax.broadcasted_iota(jnp.int32, (num_cols, num_cols), 1), 1.0, 0.0).astype(BF16)
 
-    state[...] = jnp.dot(slot_var[:ROWS], x_ref[...], precision=FULL, preferred_element_type=F32)
+    state[...] = jnp.dot(slot_var[:ROWS], x_ref[:, 0, :], precision=FULL, preferred_element_type=F32)
     mix_s[...] = lax.dot_general(eye_cols, a_ref[...], (((1,), (1,)), ((), ())),
                                  preferred_element_type=F32).astype(BF16)
     for l in range(num_layers):
-        win_s[l] = jnp.dot(win_ref[l], var_slot.astype(BF16), preferred_element_type=F32).astype(BF16)
+        win_s[l] = (0.5 * jnp.dot(win_ref[l], var_slot.astype(BF16), preferred_element_type=F32)).astype(BF16)
         wout_s[l] = jnp.dot(slot_var[:ROWS].astype(BF16), wout_ref[l], preferred_element_type=F32).astype(BF16)
 
     send1_rows = send1.reshape(num_cols, LANES)
@@ -118,6 +116,32 @@
     def settle(src, dst, ss, rs):
         pltpu.make_async_copy(src.at[pl.ds(0, num_dev - 1)], dst.at[pl.ds(0, num_dev - 1)], ss).wait()
         pltpu.make_async_copy(src.at[pl.ds(0, num_dev - 1)], dst.at[pl.ds(0, num_dev - 1)], rs).wait()
+
+    def place_lanes():
+        wide[...] = jnp.zeros_like(wide)
+        for j in range(blk):
+            wide[j, :num_cycles, :num_obs] = y_in[:, j, :]
+        for o in range(2 * halo + 1):
+            wide[blk + o, :blk, :num_obs] = r_in[o]
+        full = wide[0]
+        for j in range(1, blk):
+            full = full + pltpu.roll(wide[j], j * num_obs, 1)
+        y_ref[...] = full[:num_cycles]
+        row = lax.broadcasted_iota(jnp.int32, (8, LANES), 0)
+        full = jnp.zeros((8, LANES), F32)
+        for j in range(blk):
+            for o in range(2 * halo + 1):
+                col = j + o - halo
+                if col < 0:
+                    at = PREV_LANE + (col + halo) * num_obs
+                elif col < blk:
+                    at = col * num_obs
+                else:
+                    at = NEXT_LANE + (col - blk) * num_obs
+                moved = wide[blk + o] if at == 0 else pltpu.roll(wide[blk + o], at, 1)
+                full = full + jnp.where(row == j, moved, 0.0)
+        r_ref[...] = full
+    place_lanes()
 
     def y_copies():
         right = lax.rem(me + 1, num_dev)
@@ -127,15 +151,20 @@
                 pltpu.make_async_remote_copy(src_ref=y_ref, dst_ref=ynext, send_sem=sy1, recv_sem=ry1,
                                              device_id={'ens': left}, device_id_type=MESH))
 
-    TILE = 128
+    TILE = 256
     def forecast():
         for l in range(num_layers):
             mixed = dot32(state[...].astype(BF16), mix_s[...]).astype(BF16)
             mixed = jnp.concatenate([mixed, jnp.zeros((LANES - ROWS, num_cols), BF16)], axis=0)
             acts = []
-            for t in range(win_s.shape[1] // TILE):
-                acts.append(gelu(dot32(win_s[l, pl.ds(t * TILE, TILE), :], mixed)).astype(BF16))
-            state[...] += dot32(wout_s[l], jnp.concatenate(acts, axis=0))
+            for c in range(num_cols // TILE):
+                hidden = []
+                for t in range(win_s.shape[1] // TILE):
+                    half = dot32(win_s[l, pl.ds(t * TILE, TILE), :], mixed[:, c * TILE:(c + 1) * TILE])
+                    hidden.append(gelu_of_double(half).astype(BF16))
+                acts.append(jnp.concatenate(hidden, axis=0))
+            for c in range(num_cols // TILE):
+                state[:, c * TILE:(c + 1) * TILE] += dot32(wout_s[l], acts[c])
 
     own_col = lax.broadcasted_iota(jnp.int32, (num_obs, num_cols), 1) % blk
 
@@ -167,39 +196,40 @@
         obs_mean = jnp.mean(obs_raw, axis=0, keepdims=True)
         pert = obs_raw - obs_mean
         innov = yall[pl.ds(cycle, 1), :] - obs_mean
-        r_all = r_ref[...]
+        r_all = r_ref[:blk, :]
         energy = jnp.sum(pert * pert, axis=0, keepdims=True)
         base = (num_mem - 1) / INFLATION
         trace = num_mem * base + jnp.sum(r_all * energy, axis=1, keepdims=True)
         innov_rows = jnp.where(lax.broadcasted_iota(jnp.int32, (LANES, LANES), 0) == GAIN_LANE, innov, 0.0)
         right = jnp.concatenate([pert, innov_rows], axis=0)
-        means = []
+        means, xs, zs = [], [], []
+        threehalf = 1.5 * eye
         for j in range(blk):
             weighted = pert * r_all[j:j + 1]
             res = lax.dot_general(weighted, right, (((1,), (1,)), ((), ())), precision=FULL, preferred_element_type=F32)
             inv = 1.0 / trace[j:j + 1]
-            xz[j, :, :LANES] = (res[:, :LANES] + base * eye) * inv
+            xs.append((res[:, :LANES] + base * eye) * (0.5 * inv))
             mean = jnp.mean(raws[j], axis=0, keepdims=True)
             means.append(mean)
-            xz[j, :, LANES:] = jnp.where(mem_lane < num_vars, raws[j] - mean, res[:, LANES:])
-
-        def ns_step(k, carry):
-            for _ in range(NS_UNROLL):
-                lhs, first = [], []
-                for j in range(blk):
-                    both = xz[j]
-                    lhs.append(lhs_pack(1.5 * eye - 0.5 * both[:, :LANES]))
-                    res = dot32(lhs[j], rhs_pack(both))
-                    xz[j, :, LANES:] = res[:, LANES:]
-                    first.append(res[:, :LANES])
-                for j in range(blk):
-                    xz[j, :, :LANES] = dot32(lhs[j], rhs_pack(first[j]))
-            return carry
-        lax.fori_loop(0, (NS_STEPS - 1) // NS_UNROLL, ns_step, 0)
+            zs.append(jnp.where(mem_lane < num_vars, raws[j] - mean, res[:, LANES:]))
+
+        for _ in range(NS_STEPS - 1):
+            lhs, first = [], []
+            for j in range(blk):
+                lhs.append(lhs_pack(threehalf - xs[j]))
+                res = dot32(lhs[j], rhs_pack(jnp.concatenate([xs[j], zs[j]], axis=1)))
+                first.append(res[:, :LANES])
+                zs[j] = res[:, LANES:]
+            for j in range(blk):
+                hi, mid, lo = split3(first[j])
+                pair = jnp.concatenate([hi, mid], axis=1)
+                wide = dot32(lhs[j][:, :2 * LANES], jnp.concatenate([pair, pair], axis=0))
+                thin = dot32(lhs[j][:, 4 * LANES:], jnp.concatenate([lo, hi], axis=0))
+                xs[j] = wide[:, :LANES] + (wide[:, LANES:] + thin)
 
         for j in range(blk):
-            factor = 1.5 * eye - 0.5 * xz[j, :, :LANES]
-            fin = dot32(lhs_pack(factor), rhs_pack(xz[j, :, LANES:]))
+            factor = threehalf - xs[j]
+            fin = dot32(lhs_pack(factor), rhs_pack(zs[j]))
             inv = 1.0 / trace[j:j + 1]
             shift = jnp.sum(fin * fin[:, GAIN_LANE:GAIN_LANE + 1], axis=0, keepdims=True) * inv
             new = means[j] + shift + (math.sqrt(num_mem - 1) * jnp.sqrt(inv)) * fin
@@ -207,12 +237,12 @@
 
     def cycle_body(cycle, carry):
         forecast()
-        pack_state()
         @pl.when(cycle == 0)
         def _():
             pl.semaphore_wait(bar, num_dev - 1)
             for copy in y_copies():
                 copy.start()
+        pack_state()
         scatter(send1, land1, s1, r1)
         @pl.when(cycle == 0)
         def _():
@@ -234,7 +264,7 @@
         return carry
     lax.fori_loop(0, num_cycles, cycle_body, 0)
 
-    out_ref[...] = jnp.dot(var_slot[:, :ROWS], state[...], precision=FULL, preferred_element_type=F32)
+    out_ref[:, 0, :] = jnp.dot(var_slot[:, :ROWS], state[...], precision=FULL, preferred_element_type=F32)
 
 
 def solution(mesh):
@@ -245,20 +275,11 @@
         num_cycles, blk, num_obs = y_blk.shape
         halo = (r_blk.shape[1] - 1) // 2
         num_layers, _, num_hid = w_in.shape
-        y_flat = jnp.pad(y_blk.reshape(num_cycles, blk * num_obs), ((0, 0), (0, LANES - blk * num_obs)))
-        spread = jnp.stack([jnp.pad(r_blk[j], ((j, blk - 1 - j), (0, 0))) for j in range(blk)])
-        spread = spread.reshape(blk, (blk + 2 * halo) * num_obs)
-        width = halo * num_obs
-        prev, own, nxt = spread[:, :width], spread[:, width:width + blk * num_obs], spread[:, width + blk * num_obs:]
-        r_all = jnp.concatenate([
-            own, jnp.zeros((blk, PREV_LANE - blk * num_obs), F32), prev,
-            jnp.zeros((blk, NEXT_LANE - PREV_LANE - width), F32), nxt,
-            jnp.zeros((blk, LANES - NEXT_LANE - width), F32)], axis=1)
         vmem = pl.BlockSpec(memory_space=pltpu.VMEM)
         block = pltpu.VMEM((num_dev, blk, LANES), F32)
         out = pl.pallas_call(
             functools.partial(kernel, num_dev, num_cycles, num_obs, halo),
-            out_shape=jax.ShapeDtypeStruct((num_vars, num_cols), F32),
+            out_shape=jax.ShapeDtypeStruct((num_vars, 1, num_cols), F32),
             in_specs=[pl.BlockSpec(memory_space=pltpu.SMEM)] + [vmem] * 6,
             out_specs=vmem,
             scratch_shapes=[
@@ -267,14 +288,16 @@
                 pltpu.VMEM((num_layers, num_hid, LANES), BF16),
                 pltpu.VMEM((num_layers, ROWS, num_hid), BF16),
                 block, block, block, block,
-                pltpu.VMEM((blk, num_dev, 2 * LANES), F32),
                 pltpu.VMEM((num_cycles, LANES), F32),
                 pltpu.VMEM((num_cycles, LANES), F32),
                 pltpu.VMEM((num_cycles, LANES), F32),
+                pltpu.VMEM((num_cycles, LANES), F32),
+                pltpu.VMEM((blk + 2 * halo + 1, 8, LANES), F32),
+                pltpu.VMEM((8, LANES), F32),
             ] + [pltpu.SemaphoreType.DMA] * 8,
             compiler_params=pltpu.CompilerParams(collective_id=0, has_side_effects=True),
-        )(obs_idx, x_blk[0].T, a_mix, jnp.swapaxes(w_in, 1, 2), jnp.swapaxes(w_out, 1, 2), y_flat, r_all)
-        return out.T[None]
+        )(obs_idx, jnp.transpose(x_blk, (2, 0, 1)), a_mix, jnp.swapaxes(w_in, 1, 2), jnp.swapaxes(w_out, 1, 2), y_blk, jnp.swapaxes(r_blk, 0, 1))
+        return jnp.transpose(out, (1, 2, 0))
 
     row_spec = P(('case', 'ens'), None, None)
     return jax.shard_map(local_run, mesh=mesh,

time: 225 us -> 208 us (0.924)
  Pallas kernels: 216 us -> 203 us
  local copies, waits for them, and re-layouts: 8.06 us -> 4.45 us
    pallas_call x1, Pallas kernels: 216 us -> 203 us  [local_run(): pl.pallas_call(functools.partial(kernel, num_dev, num_cycles, num_obs, ha...]
where the time goes in v4:
time: 208 us
  Pallas kernels  203 us (98%)
  local copies, waits for them, and re-layouts  4.45 us (2%)
    pallas_call x1, Pallas kernels, local_run(): pl.pallas_call(functools.partial(kernel, num_dev, num_cycles, num_obs, ha...  203 us
    unnamed x5, local copies, waits for them, and re-layouts  4.45 us

profile of v4, /device:TPU:1, one launch (start us, length us, event | category | flops | bytes accessed | tf_op | source)
XLA Modules:
  0.0 207.6 jit_solution(17270056758531218842)
XLA Ops:
  0.0 0.0 copy-start
  0.0 1.8 copy.11
  1.8 0.0 copy-done
  1.8 1.1 copy.8
  2.9 203.1 %shard_map.73 = f32[69,1,512]{2,1,0:T(1,128)} custom-call(s32[8]{0:T(128)} %obs_ref.1, f32[69,1,512]{2,1,0:T(1,128)} %bitcast.10, bf16[512,512]{1,0:T(8,128)(2,1)} %a_ref.1, bf16[4,512,69]{2,1,0:T(8,128)(2,1)} %bitcast.7, bf16[4,69,512]{2,1,0:T(8,128)(2,1)} %bitcast.8, f32[8,4,8]{2,1,0:T(4,128)} %y_in.1, f32[7,4,8]{2,1,0:T(4,128)} %bitcast.11), custom_call_target="tpu_custom_call" | custom-call | tf_op jit(solution)/shard_map/pallas_call | solution.py:280
  206.0 1.6 copy.13
Async XLA Ops:
  0.0 1.8 copy-start

commit v5 on v4

--- a/solution.py
+++ b/solution.py
@@ -15,8 +15,9 @@
 BF16 = jnp.bfloat16
 F32 = jnp.float32
 LANES = 128
-PREV_LANE = 72
-NEXT_LANE = 96
+PART = 24
+PART_LANE = 3 * PART
+HALO_LANE = 4 * PART
 GAIN_LANE = 127
 ROWS = 80
 
@@ -37,6 +38,14 @@
 def rhs_pack(x):
     hi, mid, lo = split3(x)
     return jnp.concatenate([hi, hi, mid, mid, lo, hi], axis=0)
+
+
+def window_lane(col, blk, num_obs):
+    if col < 0:
+        return (blk + 2 * (col + blk - 1)) * num_obs
+    if col < blk:
+        return col * num_obs
+    return (blk + 2 * (col - blk) + 1) * num_obs
 
 
 def far_first(side):
@@ -64,6 +73,8 @@
     num_layers = win_ref.shape[0]
     blk = num_cols // num_dev
     num_mem = num_dev
+    rows = blk - 1
+    land2[:, rows:, :] = jnp.zeros((num_cols // blk, 1, LANES), F32)
 
     bar = pltpu.get_barrier_semaphore()
     def greet(i, carry):
@@ -109,13 +120,15 @@
     def scatter(src, dst, ss, rs):
         for dz, dy, dx, dc in far_first(side):
             peer = z_at[dz] + y_at[dy] + x_at[dx] + c_at[dc]
-            pltpu.make_async_remote_copy(src_ref=src.at[peer], dst_ref=dst.at[me], send_sem=ss, recv_sem=rs,
+            pltpu.make_async_remote_copy(src_ref=src.at[peer, pl.ds(0, rows)], dst_ref=dst.at[me, pl.ds(0, rows)], send_sem=ss, recv_sem=rs,
                                          device_id={'ens': peer}, device_id_type=MESH).start()
-        dst[pl.ds(me, 1)] = src[pl.ds(me, 1)]
+        dst[pl.ds(me, 1), :rows] = src[pl.ds(me, 1), :rows]
 
     def settle(src, dst, ss, rs):
-        pltpu.make_async_copy(src.at[pl.ds(0, num_dev - 1)], dst.at[pl.ds(0, num_dev - 1)], ss).wait()
-        pltpu.make_async_copy(src.at[pl.ds(0, num_dev - 1)], dst.at[pl.ds(0, num_dev - 1)], rs).wait()
+        sent = src.at[pl.ds(0, num_dev - 1), pl.ds(0, rows)]
+        landed = dst.at[pl.ds(0, num_dev - 1), pl.ds(0, rows)]
+        pltpu.make_async_copy(sent, landed, ss).wait()
+        pltpu.make_async_copy(sent, landed, rs).wait()
 
     def place_lanes():
         wide[...] = jnp.zeros_like(wide)
@@ -131,13 +144,7 @@
         full = jnp.zeros((8, LANES), F32)
         for j in range(blk):
             for o in range(2 * halo + 1):
-                col = j + o - halo
-                if col < 0:
-                    at = PREV_LANE + (col + halo) * num_obs
-                elif col < blk:
-                    at = col * num_obs
-                else:
-                    at = NEXT_LANE + (col - blk) * num_obs
+                at = window_lane(j + o - halo, blk, num_obs)
                 moved = wide[blk + o] if at == 0 else pltpu.roll(wide[blk + o], at, 1)
                 full = full + jnp.where(row == j, moved, 0.0)
         r_ref[...] = full
@@ -166,33 +173,42 @@
             for c in range(num_cols // TILE):
                 state[:, c * TILE:(c + 1) * TILE] += dot32(wout_s[l], acts[c])
 
-    own_col = lax.broadcasted_iota(jnp.int32, (num_obs, num_cols), 1) % blk
+    own_col = lax.broadcasted_iota(jnp.int32, (PART, num_cols), 1) % blk
 
     def pack_state():
         obs = state[:num_obs, :]
-        before = pltpu.roll(obs, blk, 1)
-        after = pltpu.roll(obs, num_cols - blk, 1)
-        parts = [state[:PREV_LANE, :]]
-        for n in range(halo):
-            parts.append(jnp.where(own_col == (n - halo) % blk, before, 0.0))
-        for n in range(halo):
-            parts.append(jnp.where(own_col == n, after, 0.0))
-        parts.append(jnp.zeros((LANES - PREV_LANE - 2 * halo * num_obs, num_cols), F32))
-        send1_rows[...] = jnp.concatenate(parts, axis=0).T
+        spread = jnp.zeros((PART, num_cols), F32)
+        for j in range(rows):
+            part = state[j * PART:(j + 1) * PART, :]
+            spread = jnp.where(own_col == j, pltpu.roll(part, num_cols - (rows - j), 1), spread)
+        send1_rows[...] = jnp.concatenate([
+            state[:PART_LANE, :], spread, pltpu.roll(obs, rows, 1), pltpu.roll(obs, num_cols - blk, 1),
+            jnp.zeros((LANES - HALO_LANE - 2 * num_obs, num_cols), F32)], axis=0).T
+
+    def unpack_state():
+        landed = land2_rows[...].T
+        spread = landed[PART_LANE:HALO_LANE]
+        for j in range(rows):
+            part = landed[j * PART:(j + 1) * PART]
+            state[j * PART:(j + 1) * PART, :] = jnp.where(own_col == rows, pltpu.roll(spread, rows - j, 1), part)
 
     mem_lane = lax.broadcasted_iota(jnp.int32, (num_mem, LANES), 1)
 
     def analyse(cycle):
-        raws = [land1_rows[pl.ds(j, num_mem, stride=blk), :] for j in range(blk)]
-        halo_sum = raws[0]
-        for j in range(1, blk):
-            halo_sum = halo_sum + raws[j]
-        own = raws[0]
-        for j in range(1, blk):
-            own = jnp.where(mem_lane >= j * num_obs, pltpu.roll(raws[j], j * num_obs, 1), own)
-        obs_raw = jnp.where(mem_lane < blk * num_obs, own, halo_sum)
-        unused = ((mem_lane >= blk * num_obs) & (mem_lane < PREV_LANE)) | (mem_lane >= NEXT_LANE + halo * num_obs)
-        obs_raw = jnp.where(unused, 0.0, obs_raw)
+        raws = [land1_rows[pl.ds(j, num_mem, stride=blk), :] for j in range(rows)]
+        def moved(j, by):
+            return pltpu.roll(raws[j], by % LANES, 1)
+        second = moved(1, PART - PART_LANE)
+        last = jnp.where(mem_lane < PART, moved(0, -PART_LANE), second)
+        last = jnp.where(mem_lane < 2 * PART, last, moved(2, 2 * PART - PART_LANE))
+        first_halo = blk * num_obs
+        pieces = [raws[0], moved(1, num_obs), moved(2, 2 * num_obs), moved(0, 3 * num_obs - PART_LANE),
+                  moved(0, first_halo - HALO_LANE), second, moved(2, first_halo + 4 * num_obs - HALO_LANE)]
+        ends = [num_obs, 2 * num_obs, 3 * num_obs, 4 * num_obs, 6 * num_obs, 8 * num_obs, 10 * num_obs]
+        obs_raw = jnp.zeros((num_mem, LANES), F32)
+        for piece, end in reversed(list(zip(pieces, ends))):
+            obs_raw = jnp.where(mem_lane < end, piece, obs_raw)
+        raws.append(last)
         obs_mean = jnp.mean(obs_raw, axis=0, keepdims=True)
         pert = obs_raw - obs_mean
         innov = yall[pl.ds(cycle, 1), :] - obs_mean
@@ -202,11 +218,12 @@
         trace = num_mem * base + jnp.sum(r_all * energy, axis=1, keepdims=True)
         innov_rows = jnp.where(lax.broadcasted_iota(jnp.int32, (LANES, LANES), 0) == GAIN_LANE, innov, 0.0)
         right = jnp.concatenate([pert, innov_rows], axis=0)
-        means, xs, zs = [], [], []
+        means, xs, zs, news = [], [], [], []
         threehalf = 1.5 * eye
+        weighted = jnp.concatenate([pert * r_all[j:j + 1] for j in range(blk)], axis=0)
+        gram = dot32(lhs_pack(weighted), rhs_pack(right.T))
         for j in range(blk):
-            weighted = pert * r_all[j:j + 1]
-            res = lax.dot_general(weighted, right, (((1,), (1,)), ((), ())), precision=FULL, preferred_element_type=F32)
+            res = gram[j * num_mem:(j + 1) * num_mem]
             inv = 1.0 / trace[j:j + 1]
             xs.append((res[:, :LANES] + base * eye) * (0.5 * inv))
             mean = jnp.mean(raws[j], axis=0, keepdims=True)
@@ -233,7 +250,10 @@
             inv = 1.0 / trace[j:j + 1]
             shift = jnp.sum(fin * fin[:, GAIN_LANE:GAIN_LANE + 1], axis=0, keepdims=True) * inv
             new = means[j] + shift + (math.sqrt(num_mem - 1) * jnp.sqrt(inv)) * fin
-            send2_rows[pl.ds(j, num_mem, stride=blk), :] = jnp.where(mem_lane < num_vars, new, 0.0)
+            news.append(jnp.where(mem_lane < num_vars, new, 0.0))
+        for j in range(rows):
+            part = pltpu.roll(news[rows], PART_LANE - j * PART, 1)
+            send2_rows[pl.ds(j, num_mem, stride=blk), :] = jnp.where(mem_lane < PART_LANE, news[j], part)
 
     def cycle_body(cycle, carry):
         forecast()
@@ -249,18 +269,18 @@
             for copy in y_copies():
                 copy.wait()
             ylane = lax.broadcasted_iota(jnp.int32, (num_cycles, LANES), 1)
-            width = halo * num_obs
-            prev = pltpu.roll(yprev[...], PREV_LANE - (blk - halo) * num_obs, 1)
-            nxt = pltpu.roll(ynext[...], NEXT_LANE, 1)
             full = y_ref[...]
-            full = jnp.where((ylane >= PREV_LANE) & (ylane < PREV_LANE + width), prev, full)
-            full = jnp.where((ylane >= NEXT_LANE) & (ylane < NEXT_LANE + width), nxt, full)
+            for n in range(halo):
+                for col, src, at in ((n - halo, yprev, blk - halo + n), (blk + n, ynext, n)):
+                    to = window_lane(col, blk, num_obs)
+                    here = (ylane >= to) & (ylane < to + num_obs)
+                    full = jnp.where(here, pltpu.roll(src[...], (to - at * num_obs) % LANES, 1), full)
             yall[...] = full
         settle(send1, land1, s1, r1)
         analyse(cycle)
         scatter(send2, land2, s2, r2)
         settle(send2, land2, s2, r2)
-        state[...] = land2_rows[...].T[:ROWS]
+        unpack_state()
         return carry
     lax.fori_loop(0, num_cycles, cycle_body, 0)
 

time: 208 us -> 204 us (0.981)
  Pallas kernels: 203 us -> 200 us
    pallas_call x1, Pallas kernels: 203 us -> 200 us  [local_run(): pl.pallas_call(functools.partial(kernel, num_dev, num_cycles, num_obs, ha...]
where the time goes in v5:
time: 204 us
  Pallas kernels  200 us (98%)
  local copies, waits for them, and re-layouts  4.45 us (2%)
    pallas_call x1, Pallas kernels, local_run(): pl.pallas_call(functools.partial(kernel, num_dev, num_cycles, num_obs, ha...  200 us
    unnamed x5, local copies, waits for them, and re-layouts  4.45 us

profile of v5, /device:TPU:1, one launch (start us, length us, event | category | flops | bytes accessed | tf_op | source)
XLA Modules:
  0.0 204.0 jit_solution(1163137096817250964)
XLA Ops:
  0.0 0.0 copy-start
  0.0 1.8 copy.11
  1.8 0.0 copy-done
  1.8 1.1 copy.8
  2.9 199.6 %shard_map.73 = f32[69,1,512]{2,1,0:T(1,128)} custom-call(s32[8]{0:T(128)} %obs_ref.1, f32[69,1,512]{2,1,0:T(1,128)} %bitcast.10, bf16[512,512]{1,0:T(8,128)(2,1)} %a_ref.1, bf16[4,512,69]{2,1,0:T(8,128)(2,1)} %bitcast.7, bf16[4,69,512]{2,1,0:T(8,128)(2,1)} %bitcast.8, f32[8,4,8]{2,1,0:T(4,128)} %y_in.1, f32[7,4,8]{2,1,0:T(4,128)} %bitcast.11), custom_call_target="tpu_custom_call" | custom-call | tf_op jit(solution)/shard_map/pallas_call | solution.py:300
  202.4 1.6 copy.13
Async XLA Ops:
  0.0 1.8 copy-start

commit v6 on v5

--- a/solution.py
+++ b/solution.py
@@ -218,12 +218,11 @@
         trace = num_mem * base + jnp.sum(r_all * energy, axis=1, keepdims=True)
         innov_rows = jnp.where(lax.broadcasted_iota(jnp.int32, (LANES, LANES), 0) == GAIN_LANE, innov, 0.0)
         right = jnp.concatenate([pert, innov_rows], axis=0)
-        means, xs, zs, news = [], [], [], []
+        means, xs, zs = [], [], []
         threehalf = 1.5 * eye
-        weighted = jnp.concatenate([pert * r_all[j:j + 1] for j in range(blk)], axis=0)
-        gram = dot32(lhs_pack(weighted), rhs_pack(right.T))
+        right = rhs_pack(right.T)
         for j in range(blk):
-            res = gram[j * num_mem:(j + 1) * num_mem]
+            res = dot32(lhs_pack(pert * r_all[j:j + 1]), right)
             inv = 1.0 / trace[j:j + 1]
             xs.append((res[:, :LANES] + base * eye) * (0.5 * inv))
             mean = jnp.mean(raws[j], axis=0, keepdims=True)
@@ -231,29 +230,35 @@
             zs.append(jnp.where(mem_lane < num_vars, raws[j] - mean, res[:, LANES:]))
 
         for _ in range(NS_STEPS - 1):
-            lhs, first = [], []
+            pairs, firsts = [], []
             for j in range(blk):
-                lhs.append(lhs_pack(threehalf - xs[j]))
-                res = dot32(lhs[j], rhs_pack(jnp.concatenate([xs[j], zs[j]], axis=1)))
-                first.append(res[:, :LANES])
+                hi, mid, lo = split3(threehalf - xs[j])
+                res = dot32(jnp.concatenate([hi, mid, hi, mid, hi, lo], axis=1),
+                            rhs_pack(jnp.concatenate([xs[j], zs[j]], axis=1)))
+                firsts.append(res[:, :LANES])
                 zs[j] = res[:, LANES:]
+                both = jnp.concatenate([hi, mid], axis=1)
+                pairs.append((jnp.concatenate([both, both], axis=0), jnp.concatenate([lo, hi], axis=0)))
             for j in range(blk):
-                hi, mid, lo = split3(first[j])
-                pair = jnp.concatenate([hi, mid], axis=1)
-                wide = dot32(lhs[j][:, :2 * LANES], jnp.concatenate([pair, pair], axis=0))
-                thin = dot32(lhs[j][:, 4 * LANES:], jnp.concatenate([lo, hi], axis=0))
+                hi, mid, lo = split3(firsts[j])
+                wide = dot32(jnp.concatenate([hi, mid], axis=1), pairs[j][0])
+                thin = dot32(jnp.concatenate([hi, lo], axis=1), pairs[j][1])
                 xs[j] = wide[:, :LANES] + (wide[:, LANES:] + thin)
 
-        for j in range(blk):
-            factor = threehalf - xs[j]
-            fin = dot32(lhs_pack(factor), rhs_pack(zs[j]))
+        fins = [None] * blk
+        for j in [rows, *range(rows)]:
+            fins[j] = dot32(lhs_pack(threehalf - xs[j]), rhs_pack(zs[j]))
+        spread = None
+        for j in [rows, *range(rows)]:
+            fin = fins[j]
             inv = 1.0 / trace[j:j + 1]
             shift = jnp.sum(fin * fin[:, GAIN_LANE:GAIN_LANE + 1], axis=0, keepdims=True) * inv
             new = means[j] + shift + (math.sqrt(num_mem - 1) * jnp.sqrt(inv)) * fin
-            news.append(jnp.where(mem_lane < num_vars, new, 0.0))
-        for j in range(rows):
-            part = pltpu.roll(news[rows], PART_LANE - j * PART, 1)
-            send2_rows[pl.ds(j, num_mem, stride=blk), :] = jnp.where(mem_lane < PART_LANE, news[j], part)
+            new = jnp.where(mem_lane < num_vars, new, 0.0)
+            if j == rows:
+                spread = [pltpu.roll(new, PART_LANE - n * PART, 1) for n in range(rows)]
+            else:
+                send2_rows[pl.ds(j, num_mem, stride=blk), :] = jnp.where(mem_lane < PART_LANE, new, spread[j])
 
     def cycle_body(cycle, carry):
         forecast()

time: 204 us -> 201 us (0.985)
  Pallas kernels: 200 us -> 196 us
    pallas_call x1, Pallas kernels: 200 us -> 196 us  [local_run(): pl.pallas_call(functools.partial(kernel, num_dev, num_cycles, num_obs, ha...]
where the time goes in v6:
time: 201 us
  Pallas kernels  196 us (98%)
  local copies, waits for them, and re-layouts  4.45 us (2%)
    pallas_call x1, Pallas kernels, local_run(): pl.pallas_call(functools.partial(kernel, num_dev, num_cycles, num_obs, ha...  196 us
    unnamed x5, local copies, waits for them, and re-layouts  4.45 us

profile of v6, /device:TPU:1, one launch (start us, length us, event | category | flops | bytes accessed | tf_op | source)
XLA Modules:
  0.0 200.9 jit_solution(14446945792496817684)
XLA Ops:
  0.0 0.0 copy-start
  0.0 1.8 copy.11
  1.8 0.0 copy-done
  1.8 1.1 copy.8
  2.9 196.5 %shard_map.73 = f32[69,1,512]{2,1,0:T(1,128)} custom-call(s32[8]{0:T(128)} %obs_ref.1, f32[69,1,512]{2,1,0:T(1,128)} %bitcast.10, bf16[512,512]{1,0:T(8,128)(2,1)} %a_ref.1, bf16[4,512,69]{2,1,0:T(8,128)(2,1)} %bitcast.7, bf16[4,69,512]{2,1,0:T(8,128)(2,1)} %bitcast.8, f32[8,4,8]{2,1,0:T(4,128)} %y_in.1, f32[7,4,8]{2,1,0:T(4,128)} %bitcast.11), custom_call_target="tpu_custom_call" | custom-call | tf_op jit(solution)/shard_map/pallas_call | solution.py:305
  199.4 1.6 copy.13
Async XLA Ops:
  0.0 1.8 copy-start

commit v7 on v6

--- a/solution.py
+++ b/solution.py
@@ -102,7 +102,8 @@
     mix_s[...] = lax.dot_general(eye_cols, a_ref[...], (((1,), (1,)), ((), ())),
                                  preferred_element_type=F32).astype(BF16)
     for l in range(num_layers):
-        win_s[l] = (0.5 * jnp.dot(win_ref[l], var_slot.astype(BF16), preferred_element_type=F32)).astype(BF16)
+        win_s[l] = (0.5 * lax.dot_general(win_ref[l], var_slot.astype(BF16), (((0,), (0,)), ((), ())),
+                                          preferred_element_type=F32)).astype(BF16)
         wout_s[l] = jnp.dot(slot_var[:ROWS].astype(BF16), wout_ref[l], preferred_element_type=F32).astype(BF16)
 
     send1_rows = send1.reshape(num_cols, LANES)
@@ -260,34 +261,39 @@
             else:
                 send2_rows[pl.ds(j, num_mem, stride=blk), :] = jnp.where(mem_lane < PART_LANE, new, spread[j])
 
-    def cycle_body(cycle, carry):
-        forecast()
-        @pl.when(cycle == 0)
-        def _():
-            pl.semaphore_wait(bar, num_dev - 1)
-            for copy in y_copies():
-                copy.start()
-        pack_state()
-        scatter(send1, land1, s1, r1)
-        @pl.when(cycle == 0)
-        def _():
-            for copy in y_copies():
-                copy.wait()
-            ylane = lax.broadcasted_iota(jnp.int32, (num_cycles, LANES), 1)
-            full = y_ref[...]
-            for n in range(halo):
-                for col, src, at in ((n - halo, yprev, blk - halo + n), (blk + n, ynext, n)):
-                    to = window_lane(col, blk, num_obs)
-                    here = (ylane >= to) & (ylane < to + num_obs)
-                    full = jnp.where(here, pltpu.roll(src[...], (to - at * num_obs) % LANES, 1), full)
-            yall[...] = full
-        settle(send1, land1, s1, r1)
+    def rest(cycle):
         analyse(cycle)
         scatter(send2, land2, s2, r2)
         settle(send2, land2, s2, r2)
         unpack_state()
+
+    def cycle_body(cycle, carry):
+        forecast()
+        pack_state()
+        scatter(send1, land1, s1, r1)
+        settle(send1, land1, s1, r1)
+        rest(cycle)
         return carry
-    lax.fori_loop(0, num_cycles, cycle_body, 0)
+
+    forecast()
+    pl.semaphore_wait(bar, num_dev - 1)
+    for copy in y_copies():
+        copy.start()
+    pack_state()
+    scatter(send1, land1, s1, r1)
+    for copy in y_copies():
+        copy.wait()
+    ylane = lax.broadcasted_iota(jnp.int32, (num_cycles, LANES), 1)
+    full = y_ref[...]
+    for n in range(halo):
+        for col, src, at in ((n - halo, yprev, blk - halo + n), (blk + n, ynext, n)):
+            to = window_lane(col, blk, num_obs)
+            here = (ylane >= to) & (ylane < to + num_obs)
+            full = jnp.where(here, pltpu.roll(src[...], (to - at * num_obs) % LANES, 1), full)
+    yall[...] = full
+    settle(send1, land1, s1, r1)
+    rest(0)
+    lax.fori_loop(1, num_cycles, cycle_body, 0)
 
     out_ref[:, 0, :] = jnp.dot(var_slot[:, :ROWS], state[...], precision=FULL, preferred_element_type=F32)
 
@@ -321,7 +327,7 @@
                 pltpu.VMEM((8, LANES), F32),
             ] + [pltpu.SemaphoreType.DMA] * 8,
             compiler_params=pltpu.CompilerParams(collective_id=0, has_side_effects=True),
-        )(obs_idx, jnp.transpose(x_blk, (2, 0, 1)), a_mix, jnp.swapaxes(w_in, 1, 2), jnp.swapaxes(w_out, 1, 2), y_blk, jnp.swapaxes(r_blk, 0, 1))
+        )(obs_idx, jnp.transpose(x_blk, (2, 0, 1)), a_mix, w_in, jnp.swapaxes(w_out, 1, 2), y_blk, jnp.swapaxes(r_blk, 0, 1))
         return jnp.transpose(out, (1, 2, 0))
 
     row_spec = P(('case', 'ens'), None, None)

time: 201 us -> 200 us (level)
  no operation moved by 1% of the time
where the time goes in v7:
time: 200 us
  Pallas kernels  196 us (98%)
  local copies, waits for them, and re-layouts  4.1 us (2%)
    pallas_call x1, Pallas kernels, local_run(): pl.pallas_call(functools.partial(kernel, num_dev, num_cycles, num_obs, ha...  196 us
    unnamed x5, local copies, waits for them, and re-layouts  4.1 us

profile of v7, /device:TPU:1, one launch (start us, length us, event | category | flops | bytes accessed | tf_op | source)
XLA Modules:
  0.0 200.0 jit_solution(17202231421228448608)
XLA Ops:
  0.0 0.0 copy-start
  0.0 1.8 copy.9.win_ref
  1.8 0.0 copy-done
  1.8 0.8 copy.11
  2.5 195.9 %shard_map.73 = f32[69,1,512]{2,1,0:T(1,128)} custom-call(s32[8]{0:T(128)} %obs_ref.1, f32[69,1,512]{2,1,0:T(1,128)} %bitcast.8, bf16[512,512]{1,0:T(8,128)(2,1)} %a_ref.1, bf16[4,69,512]{2,1,0:T(8,128)(2,1)} %copy.9.win_ref, bf16[4,69,512]{2,1,0:T(8,128)(2,1)} %bitcast.6, f32[8,4,8]{2,1,0:T(4,128)} %y_in.1, f32[7,4,8]{2,1,0:T(4,128)} %bitcast.9), custom_call_target="tpu_custom_call" | custom-call | tf_op jit(solution)/shard_map/pallas_call | solution.py:311
  198.5 1.6 copy.13
Async XLA Ops:
  0.0 1.8 copy-start
